TPU v7x, 32 devices: a whole 2x2x4 slice. The times are simulated.
32 devices in a mesh: heads: 4 (over y, core), tokens: 4 (over z), cols: 2 (over x).
Axes of the slice: x: 2, y: 2, z: 4, core: 2. Of those that a mesh axis runs over, the one named last changes fastest.
Arguments:
- query_in: bfloat16 [2048, 8192], P('tokens', ('heads', 'cols')), may hold values from -24 to 24
- key_in: bfloat16 [2048, 8192], P('tokens', ('heads', 'cols')), may hold values from -24 to 24
- value_in: bfloat16 [2048, 8192], P('tokens', ('heads', 'cols')), may hold values from -6 to 6
- out_grads: bfloat16 [2048, 8192], P('tokens', ('heads', 'cols')), may hold values from -6 to 6
- doc_starts: int32 [6], replicated, may hold values from 0 to 2047, as said below
Outputs:
- input_factor: float32 [8192, 8192], P('heads', ('tokens', 'cols'))
- grad_factor: float32 [8192, 8192], P('heads', ('tokens', 'cols'))
Inputs may be any that keep to these rules, and one draw needn't show every extreme that they name: Strictly increasing with the first entry 0; document d runs from doc_starts[d] to the next start (the last one to 2048) - 1. One document holds (4 // 2 + 1) * 512 tokens.
All inputs are finite; a program needn't handle non-finite values.
Results may differ from a plain program's by a relative error of at most 0.0041.
Values may be sent and summed in bfloat16 or wider, within the bound.
A program may use at most 128 MiB of HBM per device.

v0:
```python
import math
import jax
import jax.numpy as jnp
from jax import lax
from jax.sharding import PartitionSpec as P

HEAD_DIM = 128
MASK_FLOOR = -1e30


def spread(value, axis, source):
    kept = jnp.where(lax.axis_index(axis) == source, value, 0).astype(value.dtype)
    return lax.psum(kept, axis)


def document_ids(positions, doc_starts):
    return jnp.sum((positions[:, None] >= doc_starts[None, :]).astype(jnp.int32), axis=1) - 1


def pair_scores(query_rows, key_rows, query_pos, key_pos, doc_starts):
    head_count = query_rows.shape[1] // HEAD_DIM
    query_heads = query_rows.reshape(query_rows.shape[0], head_count, HEAD_DIM)
    key_heads = key_rows.reshape(key_rows.shape[0], head_count, HEAD_DIM)
    scores = jnp.einsum(
        "qhd,khd->hqk", query_heads, key_heads, preferred_element_type=jnp.float32
    ) * (1.0 / math.sqrt(HEAD_DIM))
    query_docs = document_ids(query_pos, doc_starts)
    key_docs = document_ids(key_pos, doc_starts)
    allowed = query_docs[:, None] == key_docs[None, :]
    return (scores, allowed[None, :, :])


def on_device(query_in, key_in, value_in, out_grads, doc_starts):
    tok_dev, row_width = query_in.shape
    head_count = row_width // HEAD_DIM
    first_pos = lax.axis_index("tokens") * tok_dev
    query_pos = first_pos + jnp.arange(tok_dev, dtype=jnp.int32)
    keys_all, values_all = (
        lax.all_gather(key_in, "tokens", axis=0, tiled=True),
        lax.all_gather(value_in, "tokens", axis=0, tiled=True),
    )
    all_tokens = keys_all.shape[0]
    key_span = min(512, all_tokens)
    block_ids = jnp.arange(all_tokens // key_span, dtype=jnp.int32)

    def block_scores(block_id):
        key_begin = block_id * key_span
        key_rows = lax.dynamic_slice_in_dim(keys_all, key_begin, key_span, 0)
        key_pos = key_begin + jnp.arange(key_span, dtype=jnp.int32)
        scores, allowed = pair_scores(query_in, key_rows, query_pos, key_pos, doc_starts)
        return (key_begin, scores, allowed)

    def gated(block_id, update, running):
        key_begin = block_id * key_span
        return update(running)

    def stats_step(running, block_id):

        def update(state):
            row_peak, row_mass = state
            key_begin, scores, allowed = block_scores(block_id)
            masked = jnp.where(allowed, scores, MASK_FLOOR)
            new_peak = jnp.maximum(row_peak, jnp.max(masked, axis=2))
            new_mass = row_mass * jnp.exp(row_peak - new_peak) + jnp.sum(
                jnp.where(allowed, jnp.exp(masked - new_peak[:, :, None]), 0.0), axis=2
            )
            return (new_peak, new_mass)

        return (gated(block_id, update, running), None)

    initial = (
        jnp.full((head_count, tok_dev), MASK_FLOOR, jnp.float32),
        jnp.zeros((head_count, tok_dev), jnp.float32),
    )
    (row_peak, row_mass), _ = lax.scan(stats_step, initial, block_ids)
    log_total = row_peak + jnp.log(row_mass)

    def value_step(running, block_id):

        def update(state):
            weighted, partials = state
            key_begin, scores, allowed = block_scores(block_id)
            weights = jnp.where(allowed, jnp.exp(scores - log_total[:, :, None]), 0.0).astype(
                jnp.bfloat16
            )
            value_rows = lax.dynamic_slice_in_dim(values_all, key_begin, key_span, 0).reshape(
                key_span, head_count, HEAD_DIM
            )
            weighted = weighted + jnp.einsum(
                "hqk,khd->qhd", weights, value_rows, preferred_element_type=jnp.float32
            )
            return (weighted, partials)

        return (gated(block_id, update, running), None)

    partial_rows = 8
    value_init = (
        jnp.zeros((tok_dev, head_count, HEAD_DIM), jnp.float32),
        jnp.zeros((partial_rows, row_width), jnp.float32),
    )
    (weighted, partials), _ = lax.scan(value_step, value_init, block_ids)
    attended = weighted.reshape(tok_dev, row_width).astype(jnp.bfloat16)
    stats_all = lax.all_gather(log_total.T, "tokens", axis=0, tiled=True)
    query_rows = lax.all_gather(query_in, "tokens", axis=0, tiled=True)
    grad_rows = lax.all_gather(out_grads, "tokens", axis=0, tiled=True)
    piece_rows = query_rows.shape[0]
    piece_pos = jnp.arange(piece_rows, dtype=jnp.int32)

    def update(grad_sum):
        scores, allowed = pair_scores(query_rows, key_in, piece_pos, query_pos, doc_starts)
        weights = jnp.where(allowed, jnp.exp(scores - stats_all.T[:, :, None]), 0.0).astype(
            jnp.bfloat16
        )
        piece_grads = grad_rows.reshape(piece_rows, head_count, HEAD_DIM)
        return jnp.einsum("hqk,qhd->khd", weights, piece_grads, preferred_element_type=jnp.float32)

    summed = update(jnp.zeros((tok_dev, head_count, HEAD_DIM), jnp.float32))
    value_grads = summed.reshape(tok_dev, row_width).astype(jnp.bfloat16)
    token_shards = lax.axis_size("tokens")
    col_shards = lax.axis_size("cols")
    rows_attended, rows_grads = (
        lax.all_gather(attended[None], ("tokens", "cols"), axis=0, tiled=True),
        lax.all_gather(value_grads[None], ("tokens", "cols"), axis=0, tiled=True),
    )
    rows_attended = rows_attended.reshape(token_shards, col_shards, tok_dev, row_width)
    rows_grads = rows_grads.reshape(token_shards, col_shards, tok_dev, row_width)
    own_attended = lax.dynamic_index_in_dim(
        rows_attended, lax.axis_index("cols"), 1, keepdims=False
    )
    own_grads = lax.dynamic_index_in_dim(rows_grads, lax.axis_index("cols"), 1, keepdims=False)
    cols_attended, cols_grads = (
        spread(own_attended, "heads", lax.axis_index("tokens")),
        spread(own_grads, "heads", lax.axis_index("tokens")),
    )
    input_factor = jnp.einsum(
        "acnf,ang->cfg", rows_attended, cols_attended, preferred_element_type=jnp.float32
    )
    grad_factor = jnp.einsum(
        "acnf,ang->cfg", rows_grads, cols_grads, preferred_element_type=jnp.float32
    )
    input_factor = input_factor.reshape(col_shards * row_width, row_width) / all_tokens
    grad_factor = grad_factor.reshape(col_shards * row_width, row_width) / all_tokens
    return (input_factor, grad_factor)


def solution(mesh):
    in_specs = (
        P("tokens", ("heads", "cols")),
        P("tokens", ("heads", "cols")),
        P("tokens", ("heads", "cols")),
        P("tokens", ("heads", "cols")),
        P(),
    )
    out_specs = (P("heads", ("tokens", "cols")), P("heads", ("tokens", "cols")))
    return jax.shard_map(
        on_device, mesh=mesh, in_specs=in_specs, out_specs=out_specs, check_vma=False
    )
```

profile of v0, /device:TPU:0, one launch (start us, length us, event | category | flops | bytes accessed | tf_op | source)
XLA Modules:
  0.0 775.8 jit_solution(3249628128545039161)
XLA Ops:
  7.2 2.4 copy.58
  9.7 2.3 copy.57
  12.8 2.3 copy.62
  15.1 78.1 %all-gather.9.cloned.1.call-done = bf16[2048,1024]{0,1:T(8,128)(2,1)} async-done(((bf16[512,1024]{0,1:T(8,128)(2,1)}), bf16[2048,1024]{0,1:T(8,128)(2,1)}) %all-gather.9.cloned.1.call-update) | async-done | bytes 4194320 | tf_op jit(solution)/shard_map/all_gather | solution.py:39
  93.2 27.0 %while.30 = (s32[]{:T(128)}, f32[8,512]{1,0:T(8,128)S(1)}, f32[8,512]{1,0:T(8,128)S(1)}, s32[6]{0:T(128)S(1)}, s32[4]{0:T(128)S(1)}, /*index=5*/bf16[2048,1024]{...) while((s32[]{:T(128)}, f32[8,512]{1,0:T(8,128)S(1)}, ...), condition=%wide.region_5.6_spmd.clone, body=%wide.region_0.5_spmd.clone.sunk | while | flops 553950208 | bytes 21995748 | solution.py:75
  96.1 1.7 fusion.59
  97.9 2.0 select_reduce_fusion.2
  104.7 2.0 select_reduce_fusion.2
  111.4 2.0 select_reduce_fusion.2
  118.2 2.0 select_reduce_fusion.2
  120.3 54.3 %all-gather.7.cloned.1.call-done = bf16[2048,1024]{0,1:T(8,128)(2,1)} async-done(((bf16[512,1024]{0,1:T(8,128)(2,1)}), bf16[2048,1024]{0,1:T(8,128)(2,1)}) %all-gather.7.cloned.1.call-update) | async-done | bytes 4194320 | tf_op jit(solution)/shard_map/all_gather | solution.py:40
  174.6 34.2 %while.31 = (s32[]{:T(128)}, f32[512,8,128]{0,2,1:T(8,128)}, s32[4]{0:T(128)S(1)}, bf16[2048,1024]{0,1:T(8,128)(2,1)}, s32[6]{0:T(128)S(1)}, /*index=5*/bf16[204...) while((s32[]{:T(128)}, f32[512,8,128]{0,2,1:T(8,128)}, ...), condition=%wide.region_9.10_spmd.clone, body=%wide.region_6.9_spmd.clone.sunk | while | flops 1083460608 | bytes 12099821 | solution.py:101
  177.9 4.0 bitcast_add_fusion.2
  183.5 1.9 constant_dynamic-slice_fusion.6
  185.4 5.6 bitcast_add_fusion.2
  194.3 5.6 bitcast_add_fusion.2
  203.2 5.6 bitcast_add_fusion.2
  208.8 1.8 convert_element_type.76
  213.0 42.4 %all-gather.15.cloned.1.call-done = bf16[2048,1024]{1,0:T(8,128)(2,1)} async-done(((bf16[512,1024]{1,0:T(8,128)(2,1)}), bf16[2048,1024]{1,0:T(8,128)(2,1)}) %all-gather.15.cloned.1.call-update) | async-done | bytes 4194320 | tf_op jit(solution)/shard_map/all_gather | solution.py:105
  255.5 6.4 copy.65
  261.9 15.2 %all_gather.25 = f32[2048,8]{0,1:T(8,128)S(1)} all-gather(f32[512,8]{0,1:T(8,128)S(1)} %bitcast.132), channel_id=1, replica_groups=mesh['heads'=4,'tokens'=4,'cols'=2] {'tokens'}, dimensions={0}, use_global_device_ids=true | all-gather | bytes 81920 | tf_op jit(solution)/shard_map/all_gather | solution.py:103
  277.1 59.8 %all-gather.13.cloned.1.call-done = bf16[2048,1024]{0,1:T(8,128)(2,1)} async-done(((bf16[512,1024]{0,1:T(8,128)(2,1)}), bf16[2048,1024]{0,1:T(8,128)(2,1)}) %all-gather.13.cloned.1.call-update) | async-done | bytes 4194320 | tf_op jit(solution)/shard_map/all_gather | solution.py:104
  336.9 14.4 %fusion.29 = bf16[8,512,128]{1,2,0:T(8,128)(2,1)S(1)} fusion(bf16[2048,8,128]{0,2,1:T(8,128)(2,1)} %bitcast.130, bf16[2048,8,128]{0,2,1:T(8,128)(2,1)} %bitcast.134, f32[8,2048]{1,0:T(8,128)S(1)} %bitcast.133, pred[2048,512]{1,0:T(8,128)(4,1)S(1)} %broadcast_compare_fusion.2, bf16[512,1024]{1,0:T(8,128)(2,1)S(1)} %copy-done.2), kind=kOutput, calls=%fused_computation.50 | convolution fusion | flops 4329046016 | bytes 11599872 | tf_op jit(solution)/shard_map/hqk,qhd->khd/dot_general | solution.py:115
  353.0 109.4 %all-gather.11.cloned.1.call-done = bf16[8,512,1024]{2,1,0:T(8,128)(2,1)} async-done(((bf16[1,512,1024]{2,1,0:T(8,128)(2,1)}), bf16[8,512,1024]{2,1,0:T(8,128)(2,1)}) %all-gather.11.cloned.1.call-update) | async-done | bytes 8388624 | tf_op jit(solution)/shard_map/all_gather | solution.py:122
  462.4 4.5 fusion.27
  466.9 120.8 %all-gather.17.cloned.1.call-done = bf16[8,512,1024]{2,1,0:T(8,128)(2,1)} async-done(((bf16[1,512,1024]{2,1,0:T(8,128)(2,1)}), bf16[8,512,1024]{2,1,0:T(8,128)(2,1)}) %all-gather.17.cloned.1.call-update) | async-done | bytes 8388624 | tf_op jit(solution)/shard_map/all_gather | solution.py:123
  587.6 4.4 fusion.26
  592.1 11.5 %copy.60 = bf16[2,1024,4,512]{3,1,0,2:T(8,128)(2,1)} copy(bf16[2,1024,4,512]{1,3,0,2:T(8,128)(2,1)} %bitcast.124) | data formatting | bytes 16777216 | tf_op jit(solution)/shard_map/acnf,ang->cfg/dot_general | solution.py:135
  603.6 11.5 %copy.67 = bf16[2,1024,4,512]{3,1,0,2:T(8,128)(2,1)} copy(bf16[2,1024,4,512]{1,3,0,2:T(8,128)(2,1)} %bitcast.126) | data formatting | bytes 16777216 | tf_op jit(solution)/shard_map/acnf,ang->cfg/dot_general | solution.py:138
  615.1 128.2 %all-reduce.3.cloned.1.call-done = (bf16[4,512,1024]{2,1,0:T(8,128)(2,1)}, bf16[4,512,1024]{2,1,0:T(8,128)(2,1)}) async-done(((bf16[4,512,1024]{2,1,0:T(8,128)(2,1)}, bf16[4,512,1024]{2,1,0:T(8,128)(2,1)}), (bf16[4,512,1024]{2,1,0:T(8,128)(2,1)}, bf16[4,512,1024]{2,1,0:T(8,128)(2,1)})) %all-reduce.3.cloned.1.call-update) | async-done | bytes 8388624 | tf_op jit(solution)/shard_map/psum | solution.py:13
  743.3 14.6 %bitcast_multiply_fusion.1 = f32[2048,1024]{1,0:T(8,128)} fusion(bf16[2048,4,512]{2,0,1:T(8,128)(2,1)} %bitcast.128, bf16[4,512,1024]{2,1,0:T(8,128)(2,1)} %get-tuple-element.383), kind=kOutput, calls=%fused_computation.43 | convolution fusion | flops 8592031744 | bytes 20971520 | tf_op jit(solution)/shard_map/acnf,ang->cfg/dot_general | solution.py:135
  757.9 11.0 %bitcast_multiply_fusion = f32[2048,1024]{1,0:T(8,128)} fusion(bf16[2048,4,512]{2,0,1:T(8,128)(2,1)S(1)} %bitcast.127, bf16[4,512,1024]{2,1,0:T(8,128)(2,1)S(1)} %copy-done.4), kind=kOutput, calls=%fused_computation.42 | convolution fusion | flops 8592031744 | bytes 20971520 | tf_op jit(solution)/shard_map/acnf,ang->cfg/dot_general | solution.py:138
  (108 shorter events, 27.9 us)
Async XLA Ops:
  7.2 86.1 %copy-start = (bf16[512,1024]{1,0:T(8,128)(2,1)S(1)}, bf16[512,1024]{1,0:T(8,128)(2,1)}, u32[]{:S(2)}) copy-start(bf16[512,1024]{1,0:T(8,128)(2,1)} %param.9) | copy-start | bytes 3145732
  7.2 86.1 %copy-start.3 = (s32[6]{0:T(128)S(1)}, s32[6]{0:T(128)}, u32[]{:S(2)}) copy-start(s32[6]{0:T(128)} %param.13) | copy-start | bytes 76
  7.2 86.0 %all-gather.9.cloned.1.call-start = ((), (), s32[]{:S(2)}) async-start(), calls=%async_computation.1 | async-start | bytes 5242880 | tf_op jit(solution)/shard_map/all_gather | solution.py:39
  9.6 165.0 %all-gather.7.cloned.1.call-start = ((), (), s32[]{:S(2)}) async-start(), calls=%async_computation | async-start | bytes 5242880 | tf_op jit(solution)/shard_map/all_gather | solution.py:40
  12.0 243.5 %all-gather.15.cloned.1.call-start = ((), (), s32[]{:S(2)}) async-start(), calls=%async_computation.4 | async-start | bytes 5242880 | tf_op jit(solution)/shard_map/all_gather | solution.py:105
  12.7 324.2 %all-gather.13.cloned.1.call-start = ((), (), s32[]{:S(2)}) async-start(), calls=%async_computation.3 | async-start | bytes 5242880 | tf_op jit(solution)/shard_map/all_gather | solution.py:104
  15.0 447.3 %all-gather.11.cloned.1.call-start = ((), (), s32[]{:S(2)}) async-start(), calls=%async_computation.2 | async-start | bytes 9437184 | tf_op jit(solution)/shard_map/all_gather | solution.py:122
  208.8 128.1 %copy-start.2 = (bf16[512,1024]{1,0:T(8,128)(2,1)S(1)}, bf16[512,1024]{1,0:T(8,128)(2,1)}, u32[]{:S(2)}) copy-start(bf16[512,1024]{1,0:T(8,128)(2,1)} %param.10) | copy-start | bytes 3145732
  212.0 375.6 %all-gather.17.cloned.1.call-start = ((), (), s32[]{:S(2)}) async-start(), calls=%async_computation.5 | async-start | bytes 9437184 | tf_op jit(solution)/shard_map/all_gather | solution.py:123
  352.7 390.6 %all-reduce.3.cloned.1.call-start = ((), (), s32[]{:S(2)}) async-start(), calls=%async_computation.6 | async-start | bytes 16777216 | tf_op jit(solution)/shard_map/psum | solution.py:13
  743.3 14.6 %copy-start.1 = (bf16[2,1024,4,512]{3,1,0,2:T(8,128)(2,1)S(1)}, bf16[2,1024,4,512]{3,1,0,2:T(8,128)(2,1)}, u32[]{:S(2)}) copy-start(bf16[2,1024,4,512]{3,1,0,2:T(8,128)(2,1)} %copy.67) | copy-start | bytes 25165828
  743.3 14.6 %copy-start.4 = (bf16[4,512,1024]{2,1,0:T(8,128)(2,1)S(1)}, bf16[4,512,1024]{2,1,0:T(8,128)(2,1)}, u32[]{:S(2)}) copy-start(bf16[4,512,1024]{2,1,0:T(8,128)(2,1)} %get-tuple-element.384) | copy-start | bytes 12582916
Sparse Core Ops, SparseCore 0:
  9.7 83.4 all-gather.8
  95.4 79.2 all-gather.6
  176.2 79.2 all-gather.14
  256.9 79.9 all-gather.12
  339.5 122.8 all-gather.10
  464.9 122.6 all-gather.16
  592.2 151.0 all-reduce.2
where the time goes:
time: 777 us; the launch traced here: 776 us
  waiting for transfers between devices  594 us (76%)
  matrix products  67.8 us (9%)
  local copies, waits for them, and re-layouts  56 us (7%)
  other arithmetic  22.4 us (3%)
  blocking collectives  15.2 us (2%)
  between operations  14.2 us (2%)
    psum x1, waiting for transfers between devices, spread(): return lax.psum(kept, axis)  128 us
    all_gather x1, waiting for transfers between devices, on_device(): lax.all_gather(value_grads[None], ('tokens', 'cols'), axis=0, tiled=True)  121 us
    all_gather x1, waiting for transfers between devices, on_device(): lax.all_gather(attended[None], ('tokens', 'cols'), axis=0, tiled=True)  109 us
    all_gather x1, waiting for transfers between devices, on_device(): lax.all_gather(key_in, 'tokens', axis=0, tiled=True)  78.1 us
    all_gather x1, waiting for transfers between devices, on_device(): query_rows = lax.all_gather(query_in, 'tokens', axis=0, tiled=True)  59.8 us
    all_gather x1, waiting for transfers between devices, on_device(): lax.all_gather(value_in, 'tokens', axis=0, tiled=True)  54.3 us
    all_gather x1, waiting for transfers between devices, on_device(): grad_rows = lax.all_gather(out_grads, 'tokens', axis=0, tiled=True)  42.4 us
    dot_general x4, matrix products, update(): jnp.einsum('hqk,khd->qhd', weights, value_rows, preferred_element_type=jn...  20.8 us
  transfers between devices with their start and end apart: 7, of which 7 were waited for; matrix products, arithmetic and copies ran while one was open for 15% of the time, Pallas kernels for 0%

commit v1 on v0

--- a/solution.py
+++ b/solution.py
@@ -101,8 +101,13 @@
     (weighted, partials), _ = lax.scan(value_step, value_init, block_ids)
     attended = weighted.reshape(tok_dev, row_width).astype(jnp.bfloat16)
     stats_all = lax.all_gather(log_total.T, "tokens", axis=0, tiled=True)
-    query_rows = lax.all_gather(query_in, "tokens", axis=0, tiled=True)
-    grad_rows = lax.all_gather(out_grads, "tokens", axis=0, tiled=True)
+    query_rows, grad_rows = jnp.split(
+        lax.all_gather(
+            jnp.concatenate([query_in, out_grads], axis=1), "tokens", axis=0, tiled=True
+        ),
+        [query_in.shape[1]],
+        axis=1,
+    )
     piece_rows = query_rows.shape[0]
     piece_pos = jnp.arange(piece_rows, dtype=jnp.int32)
 

time: 777 us -> 765 us (0.985)
  waiting for transfers between devices: 594 us -> 582 us
    all_gather x2 -> x1, waiting for transfers between devices: 102 us -> 99 us  [on_device(): lax.all_gather(jnp.concatenate([query_in, out_grads], axis=1), 'tokens',...]
  transfers between devices with their start and end apart: 7 -> 6, of which waited for: 7 -> 6; matrix products, arithmetic and copies ran while one was open for 15% -> 15% of each run, Pallas kernels for 0% -> 0%
where the time goes in v1:
time: 765 us; the launch traced here: 764 us
  waiting for transfers between devices  582 us (76%)
  matrix products  68.5 us (9%)
  local copies, waits for them, and re-layouts  54.7 us (7%)
  other arithmetic  23.8 us (3%)
  between operations  14.3 us (2%)
  blocking collectives  14.2 us (2%)
    psum x1, waiting for transfers between devices, spread(): return lax.psum(kept, axis)  128 us
    all_gather x1, waiting for transfers between devices, on_device(): lax.all_gather(value_grads[None], ('tokens', 'cols'), axis=0, tiled=True)  121 us
    all_gather x1, waiting for transfers between devices, on_device(): lax.all_gather(attended[None], ('tokens', 'cols'), axis=0, tiled=True)  102 us
    all_gather x1, waiting for transfers between devices, on_device(): lax.all_gather(jnp.concatenate([query_in, out_grads], axis=1), 'tokens',...  99 us
    all_gather x1, waiting for transfers between devices, on_device(): lax.all_gather(key_in, 'tokens', axis=0, tiled=True)  78.5 us
    all_gather x1, waiting for transfers between devices, on_device(): lax.all_gather(value_in, 'tokens', axis=0, tiled=True)  53.7 us
    dot_general x4, matrix products, update(): jnp.einsum('hqk,khd->qhd', weights, value_rows, preferred_element_type=jn...  21 us
  transfers between devices with their start and end apart: 6, of which 6 were waited for; matrix products, arithmetic and copies ran while one was open for 15% of the time, Pallas kernels for 0%

profile of v1, /device:TPU:0, one launch (start us, length us, event | category | flops | bytes accessed | tf_op | source)
XLA Modules:
  0.0 763.5 jit_solution(1116125908499573518)
XLA Ops:
  7.2 2.4 copy.58
  9.7 2.3 copy.57
  14.8 78.5 %all-gather.8.cloned.1.call-done = bf16[2048,1024]{0,1:T(8,128)(2,1)} async-done(((bf16[512,1024]{0,1:T(8,128)(2,1)}), bf16[2048,1024]{0,1:T(8,128)(2,1)}) %all-gather.8.cloned.1.call-update) | async-done | bytes 4194320 | tf_op jit(solution)/shard_map/all_gather | solution.py:39
  93.3 27.1 %while.30 = (s32[]{:T(128)}, f32[8,512]{1,0:T(8,128)S(1)}, f32[8,512]{1,0:T(8,128)S(1)}, s32[6]{0:T(128)S(1)}, s32[4]{0:T(128)S(1)}, /*index=5*/bf16[2048,1024]{...) while((s32[]{:T(128)}, f32[8,512]{1,0:T(8,128)S(1)}, ...), condition=%wide.region_5.6_spmd.clone, body=%wide.region_0.5_spmd.clone.sunk | while | flops 553950208 | bytes 21995748 | solution.py:75
  96.2 1.7 fusion.60
  98.0 2.0 select_reduce_fusion.2
  103.0 1.7 fusion.60
  104.8 2.0 select_reduce_fusion.2
  109.8 1.7 fusion.60
  111.6 2.0 select_reduce_fusion.2
  116.6 1.7 fusion.60
  118.3 2.0 select_reduce_fusion.2
  120.4 53.7 %all-gather.6.cloned.1.call-done = bf16[2048,1024]{0,1:T(8,128)(2,1)} async-done(((bf16[512,1024]{0,1:T(8,128)(2,1)}), bf16[2048,1024]{0,1:T(8,128)(2,1)}) %all-gather.6.cloned.1.call-update) | async-done | bytes 4194320 | tf_op jit(solution)/shard_map/all_gather | solution.py:40
  174.1 34.0 %while.31 = (s32[]{:T(128)}, f32[512,8,128]{0,2,1:T(8,128)}, s32[4]{0:T(128)S(1)}, bf16[2048,1024]{0,1:T(8,128)(2,1)}, s32[6]{0:T(128)S(1)}, /*index=5*/bf16[204...) while((s32[]{:T(128)}, f32[512,8,128]{0,2,1:T(8,128)}, ...), condition=%wide.region_9.10_spmd.clone, body=%wide.region_6.9_spmd.clone.sunk | while | flops 1083460608 | bytes 12099821 | solution.py:101
  177.3 4.0 bitcast_add_fusion.2
  182.8 2.1 constant_dynamic-slice_fusion.6
  184.8 5.7 bitcast_add_fusion.2
  193.7 5.6 bitcast_add_fusion.2
  202.5 5.6 bitcast_add_fusion.2
  212.2 14.2 %all_gather.22 = f32[2048,8]{0,1:T(8,128)S(1)} all-gather(f32[512,8]{0,1:T(8,128)S(1)} %bitcast.133), channel_id=1, replica_groups=mesh['heads'=4,'tokens'=4,'cols'=2] {'tokens'}, dimensions={0}, use_global_device_ids=true | all-gather | bytes 81920 | tf_op jit(solution)/shard_map/all_gather | solution.py:103
  226.4 99.0 %all-gather.12.cloned.1.call-done = bf16[2048,2048]{0,1:T(8,128)(2,1)} async-done(((bf16[512,2048]{0,1:T(8,128)(2,1)}), bf16[2048,2048]{0,1:T(8,128)(2,1)}) %all-gather.12.cloned.1.call-update) | async-done | bytes 8388624 | tf_op jit(solution)/shard_map/all_gather | solution.py:105
  325.4 6.1 fusion.36
  331.6 14.9 %fusion.29 = bf16[8,128,512]{2,1,0:T(8,128)(2,1)S(1)} fusion(bf16[2048,8,128]{0,2,1:T(8,128)(2,1)} %bitcast.131, bf16[2048,8,128]{0,2,1:T(8,128)(2,1)} %bitcast.130, f32[8,2048]{1,0:T(8,128)S(1)} %bitcast.134, pred[2048,512]{1,0:T(8,128)(4,1)S(1)} %broadcast_compare_fusion.2, bf16[512,1024]{1,0:T(8,128)(2,1)S(1)} %copy-done.3), kind=kOutput, calls=%fused_computation.51 | convolution fusion | flops 4329046016 | bytes 11599872 | tf_op jit(solution)/shard_map/hqk,qhd->khd/dot_general | solution.py:120
  348.1 102.0 %all-gather.10.cloned.1.call-done = bf16[8,512,1024]{2,1,0:T(8,128)(2,1)} async-done(((bf16[1,512,1024]{2,1,0:T(8,128)(2,1)}), bf16[8,512,1024]{2,1,0:T(8,128)(2,1)}) %all-gather.10.cloned.1.call-update) | async-done | bytes 8388624 | tf_op jit(solution)/shard_map/all_gather | solution.py:127
  450.1 4.5 fusion.27
  454.6 120.8 %all-gather.14.cloned.1.call-done = bf16[8,512,1024]{2,1,0:T(8,128)(2,1)} async-done(((bf16[1,512,1024]{2,1,0:T(8,128)(2,1)}), bf16[8,512,1024]{2,1,0:T(8,128)(2,1)}) %all-gather.14.cloned.1.call-update) | async-done | bytes 8388624 | tf_op jit(solution)/shard_map/all_gather | solution.py:128
  575.3 4.4 fusion.26
  579.8 11.5 %copy.60 = bf16[2,1024,4,512]{3,1,0,2:T(8,128)(2,1)} copy(bf16[2,1024,4,512]{1,3,0,2:T(8,128)(2,1)} %bitcast.124) | data formatting | bytes 16777216 | tf_op jit(solution)/shard_map/acnf,ang->cfg/dot_general | solution.py:140
  591.3 11.5 %copy.67 = bf16[2,1024,4,512]{3,1,0,2:T(8,128)(2,1)} copy(bf16[2,1024,4,512]{1,3,0,2:T(8,128)(2,1)} %bitcast.126) | data formatting | bytes 16777216 | tf_op jit(solution)/shard_map/acnf,ang->cfg/dot_general | solution.py:143
  602.8 128.3 %all-reduce.3.cloned.1.call-done = (bf16[4,512,1024]{2,1,0:T(8,128)(2,1)}, bf16[4,512,1024]{2,1,0:T(8,128)(2,1)}) async-done(((bf16[4,512,1024]{2,1,0:T(8,128)(2,1)}, bf16[4,512,1024]{2,1,0:T(8,128)(2,1)}), (bf16[4,512,1024]{2,1,0:T(8,128)(2,1)}, bf16[4,512,1024]{2,1,0:T(8,128)(2,1)})) %all-reduce.3.cloned.1.call-update) | async-done | bytes 8388624 | tf_op jit(solution)/shard_map/psum | solution.py:13
  731.0 14.6 %bitcast_multiply_fusion.1 = f32[2048,1024]{1,0:T(8,128)} fusion(bf16[2048,4,512]{2,0,1:T(8,128)(2,1)} %bitcast.128, bf16[4,512,1024]{2,1,0:T(8,128)(2,1)} %get-tuple-element.383), kind=kOutput, calls=%fused_computation.43 | convolution fusion | flops 8592031744 | bytes 20971520 | tf_op jit(solution)/shard_map/acnf,ang->cfg/dot_general | solution.py:140
  745.6 11.0 %bitcast_multiply_fusion = f32[2048,1024]{1,0:T(8,128)} fusion(bf16[2048,4,512]{2,0,1:T(8,128)(2,1)S(1)} %bitcast.127, bf16[4,512,1024]{2,1,0:T(8,128)(2,1)S(1)} %copy-done.5), kind=kOutput, calls=%fused_computation.42 | convolution fusion | flops 8592031744 | bytes 20971520 | tf_op jit(solution)/shard_map/acnf,ang->cfg/dot_general | solution.py:143
  (109 shorter events, 26.2 us)
Async XLA Ops:
  7.2 4.9 copy-start.2
  7.2 5.5 copy-start
  7.2 86.1 %all-gather.8.cloned.1.call-start = ((), (), s32[]{:S(2)}) async-start(), calls=%async_computation.1 | async-start | bytes 5242880 | tf_op jit(solution)/shard_map/all_gather | solution.py:39
  9.7 164.4 %all-gather.6.cloned.1.call-start = ((), (), s32[]{:S(2)}) async-start(), calls=%async_computation | async-start | bytes 5242880 | tf_op jit(solution)/shard_map/all_gather | solution.py:40
  12.0 313.4 %all-gather.12.cloned.1.call-start = ((), (), s32[]{:S(2)}) async-start(), calls=%async_computation.3 | async-start | bytes 10485760 | tf_op jit(solution)/shard_map/all_gather | solution.py:105
  12.7 80.6 %copy-start.4 = (s32[6]{0:T(128)S(1)}, s32[6]{0:T(128)}, u32[]{:S(2)}) copy-start(s32[6]{0:T(128)} %param.13) | copy-start | bytes 76
  14.7 435.4 %all-gather.10.cloned.1.call-start = ((), (), s32[]{:S(2)}) async-start(), calls=%async_computation.2 | async-start | bytes 9437184 | tf_op jit(solution)/shard_map/all_gather | solution.py:127
  211.2 364.2 %all-gather.14.cloned.1.call-start = ((), (), s32[]{:S(2)}) async-start(), calls=%async_computation.4 | async-start | bytes 9437184 | tf_op jit(solution)/shard_map/all_gather | solution.py:128
  226.4 105.2 %copy-start.3 = (bf16[512,1024]{1,0:T(8,128)(2,1)S(1)}, bf16[512,1024]{1,0:T(8,128)(2,1)}, u32[]{:S(2)}) copy-start(bf16[512,1024]{1,0:T(8,128)(2,1)} %param.10) | copy-start | bytes 3145732
  347.8 383.2 %all-reduce.3.cloned.1.call-start = ((), (), s32[]{:S(2)}) async-start(), calls=%async_computation.5 | async-start | bytes 16777216 | tf_op jit(solution)/shard_map/psum | solution.py:13
  731.0 14.6 %copy-start.1 = (bf16[2,1024,4,512]{3,1,0,2:T(8,128)(2,1)S(1)}, bf16[2,1024,4,512]{3,1,0,2:T(8,128)(2,1)}, u32[]{:S(2)}) copy-start(bf16[2,1024,4,512]{3,1,0,2:T(8,128)(2,1)} %copy.67) | copy-start | bytes 25165828
  731.0 14.6 %copy-start.5 = (bf16[4,512,1024]{2,1,0:T(8,128)(2,1)S(1)}, bf16[4,512,1024]{2,1,0:T(8,128)(2,1)}, u32[]{:S(2)}) copy-start(bf16[4,512,1024]{2,1,0:T(8,128)(2,1)} %get-tuple-element.384) | copy-start | bytes 12582916
Sparse Core Ops, SparseCore 0:
  9.8 83.4 all-gather.7
  94.9 79.2 all-gather.5
  176.3 149.0 all-gather.11
  327.4 122.6 all-gather.9
  452.7 122.6 all-gather.13
  579.9 151.0 all-reduce.2
